TPU v7x, 32 devices: a 4x2x2 block of a 4x4x8 slice. The times are simulated.
32 devices in a mesh: dp: 4 (over y, z), dcp: 8 (over x, core).
Axes of the slice: x: 4, y: 2, z: 2, core: 2. Of those that a mesh axis runs over, the one named last changes fastest.
The devices are a block of a 4x4x8 slice.
Arguments:
- q: bfloat16 [128, 128, 576], P('dp', 'dcp'), parts along dimension 0
- cache: bfloat16 [128, 128, 8, 8, 576], P('dp', None, 'dcp'), parts along dimension 0
- lens: int32 [128], P('dp'), parts along dimension 0
Outputs:
- output: bfloat16 [128, 128, 512], P('dp', 'dcp'), parts along dimension 0
There are 4 independent parts. A program takes and returns all parts, laid end to end along the dimension named above; each array names one.
All inputs are finite; a program needn't handle non-finite values.
Results may differ from a plain program's by a relative error of at most 0.00740574.
Values are sent between devices in bfloat16 or wider.
A program may use at most 768 MiB of HBM per device.

v0:
```python
import jax
import jax.numpy as jnp
from jax import lax
from jax.sharding import PartitionSpec as P

ROPE = 64
QK_DIM = 192
SCALE = QK_DIM ** -0.5


def solution(mesh):
    n = mesh.shape['dcp']

    def local(q, cache, lens):
        b, hl, k = q.shape
        r = cache.shape[1]
        page = cache.shape[3]
        lorav = k - ROPE
        d = lax.axis_index('dcp')
        qa = lax.all_gather(q, 'dcp', axis=1, tiled=True)
        c = cache.reshape(b, r * page, k)
        pos = (jnp.arange(r)[:, None] * n + d) * page + jnp.arange(page)[None, :]
        valid = pos.reshape(r * page)[None, :] < lens[:, None]
        s = jnp.einsum('bhk,btk->bht', qa, c, preferred_element_type=jnp.float32) * SCALE
        s = jnp.where(valid[:, None, :], s, -jnp.inf)
        m = jnp.max(s, axis=2)
        m = jnp.where(jnp.isfinite(m), m, 0.0)
        p = jnp.exp(s - m[:, :, None])
        l = jnp.sum(p, axis=2)
        has = l > 0.0
        lsafe = jnp.where(has, l, 1.0)
        pv = jnp.einsum('bht,btk->bhk', p.astype(jnp.bfloat16), c[:, :, :lorav], preferred_element_type=jnp.float32)
        od = (pv / lsafe[:, :, None]).astype(jnp.bfloat16)
        lse = jnp.where(has, m + jnp.log(lsafe), -jnp.inf)
        od = lax.all_to_all(od.reshape(b, n, hl, lorav), 'dcp', 1, 1, tiled=True)
        lse = lax.all_to_all(lse.reshape(b, n, hl), 'dcp', 1, 1, tiled=True)
        top = jnp.max(lse, axis=1)
        w = jnp.exp(lse - top[:, None, :])
        o = jnp.sum(w[:, :, :, None] * od.astype(jnp.float32), axis=1) / jnp.sum(w, axis=1)[:, :, None]
        return o.astype(jnp.bfloat16)

    return jax.shard_map(local, mesh=mesh, in_specs=(P('dp', 'dcp', None), P('dp', None, 'dcp', None, None), P('dp')), out_specs=P('dp', 'dcp', None), check_vma=False)
```

profile of v0, /device:TPU:81, one launch (start us, length us, event | category | flops | bytes accessed | tf_op | source)
XLA Modules:
  0.0 188.0 jit_solution(4218632984939864823)
XLA Ops:
  6.5 0.0 all-gather.2.cloned.1.call-start
  6.6 0.7 all-gather.2.cloned.1.call-update
  7.3 0.1 iota_add_fusion
  7.4 0.1 add.40
  7.5 0.0 copy-start
  7.5 51.4 %copy.11 = bf16[32,128,1,8,576]{4,3,1,0,2:T(8,128)(2,1)} copy(bf16[32,128,1,8,576]{1,4,3,2,0:T(8,128)(2,1)} %param.4) | data formatting | bytes 75497472 | tf_op args[1]
  58.9 0.0 copy-done
  58.9 0.1 broadcast_compare_fusion
  59.0 0.0 all-gather.2.cloned.1.call-done
  59.0 25.3 %fusion.2 = (f32[32,128]{1,0:T(8,128)S(1)}, f32[32,128,1024]{2,1,0:T(8,128)}) fusion(pred[32,1024]{1,0:T(8,128)(4,1)S(1)} %broadcast_compare_fusion, bf16[32,128,576]{2,1,0:T(8,128)(2,1)} %all-gather.2.cloned.1.call-done, bf16[32,128,1,8,576]{4,3,1,0,2:T(8,128)(2,1)} %copy.11), kind=kOutput, calls=%fused_computation.4 | convolution fusion | flops 4844417024 | bytes 59293696 | tf_op jit(solution)/shard_map/bhk,btk->bht/dot_general | solution.py:24
  84.3 0.1 copy.14
  84.4 8.0 %fusion.4 = f32[32,128]{1,0:T(8,128)S(1)} fusion(f32[32,128,1024]{2,1,0:T(8,128)} %get-tuple-element.8, f32[32,128]{1,0:T(8,128)S(1)} %is-finite_select_fusion.1, pred[32,1024]{1,0:T(8,128)(4,1)S(1)} %broadcast_compare_fusion), kind=kLoop, calls=%fused_computation.6 | loop fusion | flops 16773120 | bytes 16842752 | tf_op jit(solution)/shard_map/reduce_sum | solution.py:29
  92.5 0.1 copy.13
  92.6 0.7 reshape.68
  93.3 6.0 %all-to-all-start = ((f32[8,1,512]{2,1,0:T(1,128)}), f32[8,1,512]{2,1,0:T(1,128)S(1)}, u32[]{:S(2)}, u32[]{:S(2)}) async-start(f32[8,1,512]{2,1,0:T(1,128)} %reshape.68), calls=%async_computation | async-start | bytes 32768 | tf_op jit(solution)/shard_map/all_to_all | solution.py:36
  99.3 20.0 %divide_convert_fusion = bf16[32,128,512]{2,1,0:T(8,128)(2,1)} fusion(f32[32,128]{1,0:T(8,128)S(1)} %compare_select_fusion.2, bf16[32,1024,576]{2,1,0:T(8,128)(2,1)} %bitcast.14, f32[32,128,1024]{2,1,0:T(8,128)} %get-tuple-element.8, f32[32,128]{1,0:T(8,128)S(1)} %is-finite_select_fusion.1, pred[32,1024]{1,0:T(8,128)(4,1)S(1)} %broadcast_compare_fusion), kind=kOutput, calls=%fused_computation.8 | convolution fusion | flops 4315938816 | bytes 54591488 | tf_op jit(solution)/shard_map/bht,btk->bhk/dot_general | solution.py:32
  119.3 4.7 %copy.16 = bf16[32,8,16,512]{3,2,0,1:T(8,128)(2,1)} copy(bf16[32,8,16,512]{3,2,1,0:T(8,128)(2,1)} %bitcast.15) | data formatting | bytes 8388608 | tf_op jit(solution)/shard_map/reshape | solution.py:35
  124.0 0.0 all-to-all-done
  124.0 4.8 %all-to-all-start.1 = ((bf16[32,8,16,512]{3,2,0,1:T(8,128)(2,1)}), bf16[32,8,16,512]{3,2,0,1:T(8,128)(2,1)}, u32[]{:S(2)}, u32[]{:S(2)}) async-start(bf16[32,8,16,512]{3,2,0,1:T(8,128)(2,1)} %copy.16), calls=%async_computation.1 | async-start | bytes 8388608 | tf_op jit(solution)/shard_map/all_to_all | solution.py:35
  128.9 0.5 broadcast.58
  129.4 0.7 reduce
  130.1 0.1 reshape.69
  130.2 0.1 copy.15
  130.3 0.1 copy.17
  130.4 47.1 %all-to-all-done.1 = bf16[32,8,16,512]{3,2,0,1:T(8,128)(2,1)} async-done(((bf16[32,8,16,512]{3,2,0,1:T(8,128)(2,1)}), bf16[32,8,16,512]{3,2,0,1:T(8,128)(2,1)}, u32[]{:S(2)}, u32[]{:S(2)}) %all-to-all-start.1) | async-done | bytes 4194336 | tf_op jit(solution)/shard_map/all_to_all | solution.py:35
  177.4 2.8 %multiply_reduce_fusion = f32[32,16,512]{2,1,0:T(8,128)S(1)} fusion(bf16[32,8,16,512]{3,2,0,1:T(8,128)(2,1)} %all-to-all-done.1, f32[32,8,16]{2,0,1:T(8,128)S(1)} %copy.15), kind=kLoop, calls=%fused_computation.7 | loop fusion | flops 6029312 | bytes 5259264 | tf_op jit(solution)/shard_map/reduce_sum | solution.py:39
  180.2 0.9 divide_convert_fusion.1
  (6 shorter events, 0.1 us)
Async XLA Ops:
  6.5 52.4 %all-gather.2.cloned.1.call-start = ((), (), s32[]{:S(2)}) async-start(), calls=%async_computation.2 | async-start | bytes 5898240 | tf_op jit(solution)/shard_map/all_gather | solution.py:20
  7.5 51.4 %copy-start = (s32[32]{0:T(128)S(1)}, s32[32]{0:T(128)}, u32[]{:S(2)}) copy-start(s32[32]{0:T(128)} %param.5) | copy-start | bytes 388
  93.3 30.7 %all-to-all-start = ((f32[8,1,512]{2,1,0:T(1,128)}), f32[8,1,512]{2,1,0:T(1,128)S(1)}, u32[]{:S(2)}, u32[]{:S(2)}) async-start(f32[8,1,512]{2,1,0:T(1,128)} %reshape.68), calls=%async_computation | async-start | bytes 32768 | tf_op jit(solution)/shard_map/all_to_all | solution.py:36
  124.0 53.4 %all-to-all-start.1 = ((bf16[32,8,16,512]{3,2,0,1:T(8,128)(2,1)}), bf16[32,8,16,512]{3,2,0,1:T(8,128)(2,1)}, u32[]{:S(2)}, u32[]{:S(2)}) async-start(bf16[32,8,16,512]{3,2,0,1:T(8,128)(2,1)} %copy.16), calls=%async_computation.1 | async-start | bytes 8388608 | tf_op jit(solution)/shard_map/all_to_all | solution.py:35
Sparse Core Ops, SparseCore 0:
  8.9 37.5 all-gather.1
where the time goes:
time: 190 us; the launch traced here: 188 us
  local copies, waits for them, and re-layouts  57.8 us (30%)
  waiting for transfers between devices  47.8 us (25%)
  matrix products  45.3 us (24%)
  between operations  13.5 us (7%)
  other arithmetic  12.7 us (7%)
  starting transfers between devices  10.8 us (6%)
    unnamed x5, local copies, waits for them, and re-layouts  52.1 us
    all_to_all x1, waiting for transfers between devices, local(): od = lax.all_to_all(od.reshape(b, n, hl, lorav), 'dcp', 1, 1, tiled=True)  47.1 us
    dot_general x1, matrix products, local(): jnp.einsum('bhk,btk->bht', qa, c, preferred_element_type=jnp.float32)  25.3 us
    dot_general x1, matrix products, local(): jnp.einsum('bht,btk->bhk', p.astype(jnp.bfloat16), c[:, :, :lorav], prefe...  20 us
    reduce_sum x1, other arithmetic, local(): l = jnp.sum(p, axis=2)  8.03 us
    all_to_all x1, starting transfers between devices, local(): lse = lax.all_to_all(lse.reshape(b, n, hl), 'dcp', 1, 1, tiled=True)  6.02 us
    all_to_all x1, starting transfers between devices, local(): od = lax.all_to_all(od.reshape(b, n, hl, lorav), 'dcp', 1, 1, tiled=True)  4.82 us
    reshape x1, local copies, waits for them, and re-layouts, local(): od = lax.all_to_all(od.reshape(b, n, hl, lorav), 'dcp', 1, 1, tiled=True)  4.74 us
  transfers between devices with their start and end apart: 3, of which 1 were waited for; matrix products, arithmetic and copies ran while one was open for 41% of the time, Pallas kernels for 0%

commit v1 on v0

v1 whole, which is shorter than its diff:
```python
import functools

import jax
import jax.numpy as jnp
from jax import lax
from jax.experimental import pallas as pl
from jax.experimental.pallas import tpu as pltpu
from jax.sharding import PartitionSpec as P

ROPE = 64
QK_DIM = 192
C2 = QK_DIM ** -0.5 * 1.4426950408889634

G = 2
AHEAD = 3
RING = 14
PSLOT = 8
LB = 2


def kernel(n, q_hbm, c_hbm, lens_ref, o_ref, qall, cbuf, pbuf, mbuf, lse_all, obuf, xrecv, snd,
           relay_in, o_in, lsem, csem, send_sem, ql_sem, qr_sem, qd_sem, qp_sem, lse_sem, x_sem,
           a_sem, ol_sem, or_sem, od_sem):
    nseq, hl, k = q_hbm.shape
    npage, _, r = c_hbm.shape[1:]
    lorav = k - ROPE
    nx = n // 2
    half = nx * hl
    heads = n * hl
    nc = nseq // G

    me = lax.axis_index('dcp')
    x = me // 2
    core = me % 2
    right = (me + 2) % n
    left = (me + n - 2) % n
    opp = (me + 4) % n
    mate = me + 1 - 2 * core

    def row(j):
        return ((j % 2) * nx + j // 2) * hl

    def remote(src, dst, ssem, rsem, dev):
        return pltpu.make_async_remote_copy(
            src_ref=src, dst_ref=dst, send_sem=ssem, recv_sem=rsem, device_id={'dcp': dev},
            device_id_type=pl.DeviceIdType.MESH)

    def wait_on(ref, sem):
        pltpu.make_async_copy(ref, ref, sem).wait()

    def cache_copy(b):
        s = b % RING
        return pltpu.make_async_copy(c_hbm.at[b], cbuf.at[s], csem.at[s])

    def qblk(c, j):
        return qall.at[pl.ds(c * G, G), pl.ds(row(j), hl), :]

    qcopy = pltpu.make_async_copy(q_hbm, qall.at[:, pl.ds(row(me), hl), :], lsem.at[0])
    qcopy.start()
    for b in range(RING):
        cache_copy(b).start()

    barrier = pltpu.get_barrier_semaphore()
    for d in range(1, n):
        pl.semaphore_signal(barrier, inc=1, device_id={'dcp': (me + d) % n},
                            device_id_type=pl.DeviceIdType.MESH)
    pl.semaphore_wait(barrier, n - 1)
    qcopy.wait()

    def send_own(c):
        blk = qblk(c, me)
        remote(blk, blk, send_sem.at[0], ql_sem.at[c], right).start()
        remote(blk, blk, send_sem.at[1], qr_sem.at[c], left).start()
        remote(blk, blk, send_sem.at[2], qp_sem.at[c], mate).start()

    def q_first(c):
        wait_on(qblk(c, left), ql_sem.at[c])
        wait_on(qblk(c, right), qr_sem.at[c])
        even = c % 2 == 0
        blk = qblk(c, jnp.where(even, left, right))
        remote(blk, blk, send_sem.at[3], qd_sem.at[c], jnp.where(even, right, left)).start()
        for j in (left, right):
            blk = qblk(c, j)
            remote(blk, blk, send_sem.at[2], qp_sem.at[c], mate).start()

    def q_second(c):
        blk = qblk(c, opp)
        wait_on(blk, qd_sem.at[c])
        remote(blk, blk, send_sem.at[2], qp_sem.at[c], mate).start()

    def q_third(c):
        wait_on(qall.at[pl.ds(c * G, G), pl.ds((1 - core) * half, half), :], qp_sem.at[c])

    def cache_t(s):
        return cbuf[s]

    def scores(c):
        for g in range(G):
            b = c * G + g
            cache_copy(b).wait()
            ct = cbuf[b % RING]
            ct = jnp.concatenate([ct[i] for i in range(npage)], axis=1)
            s = lax.dot_general(qall[b], ct, (((1,), (0,)), ((), ())), preferred_element_type=jnp.float32)
            length = lens_ref[b] - me * npage
            posr = lax.broadcasted_iota(jnp.int32, (1, r), 1) * (n * npage)
            mask = jnp.concatenate([posr < length - i for i in range(npage)], axis=1)
            s = jnp.where(mask, s, -jnp.inf)
            m = jnp.max(s, axis=1, keepdims=True) * C2
            msafe = jnp.where(m == -jnp.inf, 0.0, m)
            p = jnp.exp2(s * C2 - msafe)
            l = jnp.sum(p, axis=1, keepdims=True)
            ps = b % PSLOT
            pbuf[ps] = p
            mbuf[ps] = m
            lse = jnp.where(l > 0.0, msafe + jnp.log2(jnp.where(l > 0.0, l, 1.0)), -jnp.inf)
            t = jnp.transpose(jnp.broadcast_to(lse, (heads, heads)))
            lse_all[me, b] = t[0:1]
        blk = lse_all.at[me, pl.ds(c * G, G)]
        for d in range(1, n):
            remote(blk, blk, send_sem.at[4], lse_sem.at[c], (me + d) % n).start()

    def product(c):
        wait_on(lse_all.at[pl.ds(0, n - 1), pl.ds(c * G, G)], lse_sem.at[c])
        for g in range(G):
            b = c * G + g
            rows = [lse_all[j, b] for j in range(n)]
            top = functools.reduce(jnp.maximum, rows)
            tot = functools.reduce(jnp.add, [jnp.exp2(z - top) for z in rows])
            big = top + jnp.log2(tot)
            bigc = jnp.transpose(jnp.broadcast_to(big, (heads, heads)))[:, 0:1]
            ps = b % PSLOT
            f = jnp.exp2(mbuf[ps] - bigc)
            a = (pbuf[ps] * f).astype(jnp.bfloat16)
            ct = cbuf[b % RING]
            ct = jnp.concatenate([ct[i, :lorav] for i in range(npage)], axis=1)
            ot = lax.dot_general(ct, a, (((1,), (1,)), ((), ())), preferred_element_type=jnp.float32)
            obuf[b] = jnp.transpose(ot)
            remote(obuf.at[b, pl.ds((1 - core) * half, half)], xrecv.at[b], send_sem.at[5], x_sem.at[c],
                   mate).start()

            @pl.when(b + RING < nseq)
            def _():
                cache_copy(b + RING).start()

    def chip_sum(c):
        bs = pl.ds(c * G, G)
        wait_on(xrecv.at[bs], x_sem.at[c])
        snd[bs] = (obuf[bs, pl.ds(core * half, half)] + xrecv[bs]).astype(jnp.bfloat16)

        def part(j):
            return snd.at[bs, pl.ds((j // 2) * hl, hl)]

        even = c % 2 == 0
        remote(part(opp), relay_in.at[bs], send_sem.at[6], a_sem.at[c], jnp.where(even, right, left)).start()
        remote(part(right), o_in.at[0, bs], send_sem.at[6], ol_sem.at[c], right).start()
        remote(part(left), o_in.at[1, bs], send_sem.at[6], or_sem.at[c], left).start()

    def relay(c):
        bs = pl.ds(c * G, G)
        wait_on(relay_in.at[bs], a_sem.at[c])
        remote(relay_in.at[bs], o_in.at[2, bs], send_sem.at[7], od_sem.at[c],
               jnp.where(c % 2 == 0, right, left)).start()

    def final(c):
        bs = pl.ds(c * G, G)
        wait_on(o_in.at[0, bs], ol_sem.at[c])
        wait_on(o_in.at[1, bs], or_sem.at[c])
        wait_on(o_in.at[2, bs], od_sem.at[c])
        own = obuf[bs, pl.ds(row(me), hl)] + xrecv[bs, pl.ds(x * hl, hl)]
        o_ref[bs] = (own + o_in[0, bs].astype(jnp.float32) + o_in[1, bs].astype(jnp.float32)
                     + o_in[2, bs].astype(jnp.float32)).astype(o_ref.dtype)

    for c in range(AHEAD):
        send_own(c)

    stages = [(q_first, 0), (q_second, 1), (q_third, 2), (scores, 2), (product, 2 + LB),
              (chip_sum, 3 + LB), (relay, 4 + LB), (final, 6 + LB)]
    last = max(d for _, d in stages)

    @pl.loop(0, nc + last)
    def _(it):
        @pl.when(it + AHEAD < nc)
        def _():
            send_own(it + AHEAD)

        for f, d in stages:
            @pl.when((it >= d) & (it < nc + d))
            def _(f=f, d=d):
                f(it - d)

    wait_on(qall.at[:, pl.ds(0, hl), :], send_sem.at[0])
    wait_on(qall.at[:, pl.ds(0, hl), :], send_sem.at[1])
    wait_on(qall.at[:, pl.ds(0, half), :], send_sem.at[2])
    wait_on(qall.at[:, pl.ds(0, hl), :], send_sem.at[3])
    wait_on(lse_all.at[pl.ds(0, n - 1)], send_sem.at[4])
    wait_on(xrecv, send_sem.at[5])
    wait_on(snd.at[:, pl.ds(0, (nx - 1) * hl)], send_sem.at[6])
    wait_on(relay_in, send_sem.at[7])


def solution(mesh):
    n = mesh.shape['dcp']

    def local(q, cache, lens):
        b, hl, k = q.shape
        r = cache.shape[1]
        page = cache.shape[3]
        lorav = k - ROPE
        ct = cache.reshape(b, r, page, k).transpose(0, 2, 3, 1)
        heads = n * hl
        half = heads // 2
        nc = b // G
        dma = pltpu.SemaphoreType.DMA
        return pl.pallas_call(
            functools.partial(kernel, n),
            out_shape=jax.ShapeDtypeStruct((b, hl, lorav), jnp.bfloat16),
            in_specs=[pl.BlockSpec(memory_space=pl.ANY), pl.BlockSpec(memory_space=pl.ANY),
                      pl.BlockSpec(memory_space=pltpu.SMEM)],
            out_specs=pl.BlockSpec(memory_space=pltpu.VMEM),
            scratch_shapes=[
                pltpu.VMEM((b, heads, k), jnp.bfloat16),
                pltpu.VMEM((RING, page, k, r), jnp.bfloat16),
                pltpu.VMEM((PSLOT, heads, r * page), jnp.float32),
                pltpu.VMEM((PSLOT, heads, 1), jnp.float32),
                pltpu.VMEM((n, b, 1, heads), jnp.float32),
                pltpu.VMEM((b, heads, lorav), jnp.float32),
                pltpu.VMEM((b, half, lorav), jnp.float32),
                pltpu.VMEM((b, half, lorav), jnp.bfloat16),
                pltpu.VMEM((b, hl, lorav), jnp.bfloat16),
                pltpu.VMEM((3, b, hl, lorav), jnp.bfloat16),
                dma((1,)), dma((RING,)), dma((8,)),
            ] + [dma((nc,))] * 10,
            compiler_params=pltpu.CompilerParams(
                collective_id=0, has_side_effects=True, vmem_limit_bytes=66_000_000),
        )(q, ct, lens)

    return jax.shard_map(local, mesh=mesh,
                         in_specs=(P('dp', 'dcp', None), P('dp', None, 'dcp', None, None), P('dp')),
                         out_specs=P('dp', 'dcp', None), check_vma=False)
```

time: 190 us -> 91.6 us (0.48)
  Pallas kernels: 0 us -> 88.9 us
  local copies, waits for them, and re-layouts: 57.8 us -> 1.87 us
  waiting for transfers between devices: 47.8 us -> 0 us
  matrix products: 45.3 us -> 0 us
  between operations: 13.5 us -> 0.01 us
  other arithmetic: 12.7 us -> 0 us
  starting transfers between devices: 10.8 us -> 0 us
    pallas_call x0 -> x1, Pallas kernels: none -> 88.9 us  [local(): pl.pallas_call(functools.partial(kernel, n), out_shape=jax.ShapeDtypeStru...]
    unnamed x5 -> x1, local copies, waits for them, and re-layouts: 52.1 us -> 1.87 us
    all_to_all x2 -> x0, waiting for transfers between devices: 47.1 us -> none  [the longest x1 47.1 us: local(): od = lax.all_to_all(od.reshape(b, n, hl, lorav), 'dcp', 1, 1, tiled=True)]
    dot_general x2 -> x0, matrix products: 45.3 us -> none  [the longest x1 25.3 us: local(): jnp.einsum('bhk,btk->bht', qa, c, preferred_element_type=jnp.float32)]
    reduce_sum x3 -> x0, other arithmetic: 10.8 us -> none  [the longest x1 8.03 us: local(): l = jnp.sum(p, axis=2)]
    all_to_all x2 -> x0, starting transfers between devices: 10.8 us -> none  [the longest x1 6.02 us: local(): lse = lax.all_to_all(lse.reshape(b, n, hl), 'dcp', 1, 1, tiled=True)]
    reshape x1 -> x0, local copies, waits for them, and re-layouts: 4.74 us -> none  [local(): od = lax.all_to_all(od.reshape(b, n, hl, lorav), 'dcp', 1, 1, tiled=True)]
  transfers between devices with their start and end apart: 3 -> 0, of which waited for: 1 -> 0; matrix products, arithmetic and copies ran while one was open for 41% -> 0% of each run, Pallas kernels for 0% -> 0%
where the time goes in v1:
time: 91.6 us; the launch traced here: 90.8 us
  Pallas kernels  88.9 us (97%)
  local copies, waits for them, and re-layouts  1.87 us (2%)
    pallas_call x1, Pallas kernels, local(): pl.pallas_call(functools.partial(kernel, n), out_shape=jax.ShapeDtypeStru...  88.9 us
    unnamed x1, local copies, waits for them, and re-layouts  1.87 us

profile of v1, /device:TPU:81, one launch (start us, length us, event | category | flops | bytes accessed | tf_op | source)
XLA Modules:
  0.0 90.8 jit_solution(14603102252039026363)
XLA Ops:
  0.0 88.9 %shard_map.37 = bf16[32,16,512]{2,1,0:T(8,128)(2,1)} custom-call(bf16[32,16,576]{2,1,0:T(8,128)(2,1)} %q_hbm.1, bf16[32,8,576,128]{3,2,1,0:T(8,128)(2,1)} %bitcast.3, s32[32]{0:T(128)} %lens_ref.1), custom_call_target="tpu_custom_call" | custom-call | tf_op jit(solution)/shard_map/pallas_call | solution.py:214
  88.9 1.9 %copy.5 = bf16[32,16,512]{2,1,0:T(8,128)(2,1)} copy(bf16[32,16,512]{2,1,0:T(8,128)(2,1)} %shard_map.37) | data formatting | bytes 1048576

commit v2 on v1

--- a/solution.py
+++ b/solution.py
@@ -12,10 +12,17 @@
 C2 = QK_DIM ** -0.5 * 1.4426950408889634
 
 G = 2
-AHEAD = 3
+AHEAD = 2
 RING = 14
 PSLOT = 8
-LB = 2
+D_Q2 = 2
+D_Q3 = 4
+D_SC = 4
+D_PR = 7
+D_CS = 9
+D_RL = 12
+D_FI = 16
+NT = True
 
 
 def kernel(n, q_hbm, c_hbm, lens_ref, o_ref, qall, cbuf, pbuf, mbuf, lse_all, obuf, xrecv, snd,
@@ -91,13 +98,9 @@
     def q_third(c):
         wait_on(qall.at[pl.ds(c * G, G), pl.ds((1 - core) * half, half), :], qp_sem.at[c])
 
-    def cache_t(s):
-        return cbuf[s]
-
     def scores(c):
         for g in range(G):
             b = c * G + g
-            cache_copy(b).wait()
             ct = cbuf[b % RING]
             ct = jnp.concatenate([ct[i] for i in range(npage)], axis=1)
             s = lax.dot_general(qall[b], ct, (((1,), (0,)), ((), ())), preferred_element_type=jnp.float32)
@@ -115,12 +118,8 @@
             lse = jnp.where(l > 0.0, msafe + jnp.log2(jnp.where(l > 0.0, l, 1.0)), -jnp.inf)
             t = jnp.transpose(jnp.broadcast_to(lse, (heads, heads)))
             lse_all[me, b] = t[0:1]
-        blk = lse_all.at[me, pl.ds(c * G, G)]
-        for d in range(1, n):
-            remote(blk, blk, send_sem.at[4], lse_sem.at[c], (me + d) % n).start()
 
     def product(c):
-        wait_on(lse_all.at[pl.ds(0, n - 1), pl.ds(c * G, G)], lse_sem.at[c])
         for g in range(G):
             b = c * G + g
             rows = [lse_all[j, b] for j in range(n)]
@@ -133,10 +132,30 @@
             a = (pbuf[ps] * f).astype(jnp.bfloat16)
             ct = cbuf[b % RING]
             ct = jnp.concatenate([ct[i, :lorav] for i in range(npage)], axis=1)
-            ot = lax.dot_general(ct, a, (((1,), (1,)), ((), ())), preferred_element_type=jnp.float32)
-            obuf[b] = jnp.transpose(ot)
-            remote(obuf.at[b, pl.ds((1 - core) * half, half)], xrecv.at[b], send_sem.at[5], x_sem.at[c],
-                   mate).start()
+            if NT:
+                obuf[b] = lax.dot_general(a, ct, (((1,), (1,)), ((), ())), preferred_element_type=jnp.float32)
+            else:
+                ot = lax.dot_general(ct, a, (((1,), (1,)), ((), ())), preferred_element_type=jnp.float32)
+                obuf[b] = jnp.transpose(ot)
+
+    def scores_wait(c):
+        for g in range(G):
+            cache_copy(c * G + g).wait()
+
+    def product_wait(c):
+        wait_on(lse_all.at[pl.ds(0, n - 1), pl.ds(c * G, G)], lse_sem.at[c])
+
+    def scores_send(c):
+        blk = lse_all.at[me, pl.ds(c * G, G)]
+        for d in range(1, n):
+            remote(blk, blk, send_sem.at[4], lse_sem.at[c], (me + d) % n).start()
+
+    def product_send(c):
+        bs = pl.ds(c * G, G)
+        remote(obuf.at[bs, pl.ds((1 - core) * half, half)], xrecv.at[bs], send_sem.at[5], x_sem.at[c],
+               mate).start()
+        for g in range(G):
+            b = c * G + g
 
             @pl.when(b + RING < nseq)
             def _():
@@ -173,20 +192,45 @@
     for c in range(AHEAD):
         send_own(c)
 
-    stages = [(q_first, 0), (q_second, 1), (q_third, 2), (scores, 2), (product, 2 + LB),
-              (chip_sum, 3 + LB), (relay, 4 + LB), (final, 6 + LB)]
-    last = max(d for _, d in stages)
-
-    @pl.loop(0, nc + last)
-    def _(it):
+    def step(it, do_scores, do_product):
+        def stage(f, d):
+            @pl.when((it >= d) & (it < nc + d))
+            def _():
+                f(it - d)
+
         @pl.when(it + AHEAD < nc)
         def _():
             send_own(it + AHEAD)
 
-        for f, d in stages:
-            @pl.when((it >= d) & (it < nc + d))
-            def _(f=f, d=d):
-                f(it - d)
+        stage(q_first, 0)
+        stage(q_second, D_Q2)
+        stage(q_third, D_Q3)
+        stage(chip_sum, D_CS)
+        stage(relay, D_RL)
+        stage(final, D_FI)
+        if do_scores:
+            scores_wait(it - D_SC)
+        if do_product:
+            product_wait(it - D_PR)
+        if do_scores:
+            scores(it - D_SC)
+        if do_product:
+            product(it - D_PR)
+        if do_scores:
+            scores_send(it - D_SC)
+        if do_product:
+            product_send(it - D_PR)
+
+    def run(lo, hi, do_scores, do_product):
+        @pl.loop(lo, hi)
+        def _(it):
+            step(it, do_scores, do_product)
+
+    run(0, D_SC, False, False)
+    run(D_SC, D_PR, True, False)
+    run(D_PR, nc + D_SC, True, True)
+    run(nc + D_SC, nc + D_PR, False, True)
+    run(nc + D_PR, nc + D_FI, False, False)
 
     wait_on(qall.at[:, pl.ds(0, hl), :], send_sem.at[0])
     wait_on(qall.at[:, pl.ds(0, hl), :], send_sem.at[1])

time: 91.6 us -> 67.7 us (0.74)
  Pallas kernels: 88.9 us -> 65.6 us
    pallas_call x1, Pallas kernels: 88.9 us -> 65.6 us  [local(): pl.pallas_call(functools.partial(kernel, n), out_shape=jax.ShapeDtypeStru...]
where the time goes in v2:
time: 67.7 us; the launch traced here: 67.5 us
  Pallas kernels  65.6 us (97%)
  local copies, waits for them, and re-layouts  1.87 us (3%)
    pallas_call x1, Pallas kernels, local(): pl.pallas_call(functools.partial(kernel, n), out_shape=jax.ShapeDtypeStru...  65.6 us
    unnamed x1, local copies, waits for them, and re-layouts  1.87 us

profile of v2, /device:TPU:81, one launch (start us, length us, event | category | flops | bytes accessed | tf_op | source)
XLA Modules:
  0.0 67.5 jit_solution(7865040602123682672)
XLA Ops:
  0.0 65.6 %shard_map.37 = bf16[32,16,512]{2,1,0:T(8,128)(2,1)} custom-call(bf16[32,16,576]{2,1,0:T(8,128)(2,1)} %q_hbm.1, bf16[32,8,576,128]{3,2,1,0:T(8,128)(2,1)} %bitcast.3, s32[32]{0:T(128)} %lens_ref.1), custom_call_target="tpu_custom_call" | custom-call | tf_op jit(solution)/shard_map/pallas_call | solution.py:258
  65.7 1.9 %copy.5 = bf16[32,16,512]{2,1,0:T(8,128)(2,1)} copy(bf16[32,16,512]{2,1,0:T(8,128)(2,1)} %shard_map.37) | data formatting | bytes 1048576

commit v3 on v1

v3 whole, which is shorter than its diff:
```python
import functools

import jax
import jax.numpy as jnp
from jax import lax
from jax.experimental import pallas as pl
from jax.experimental.pallas import tpu as pltpu
from jax.sharding import PartitionSpec as P

ROPE = 64
QK_DIM = 192
C2 = QK_DIM ** -0.5 * 1.4426950408889634

G = 2
GQ = 2
AHEAD = 4
RING = 14
PSLOT = 8
LEAD = 3
EARLY = 2
D_Q2 = 4
D_Q3 = 6
D_SC = 6
D_PR = 8
D_CS = 10
D_RL = 14
D_FI = 19
NT = True


def kernel(n, q_hbm, c_hbm, lens_ref, o_ref, qall, cbuf, pbuf, abuf, mbuf, lse_own, lse_mate, lse_chip, lse_in, wt, obuf, xrecv, snd,
           relay_in, o_in, lsem, csem, send_sem, ql_sem, qr_sem, qd_sem, qp_sem, lse_sem, lc_sem, x_sem,
           a_sem, ol_sem, or_sem, od_sem):
    nseq, hl, k = q_hbm.shape
    npage, _, r = c_hbm.shape[1:]
    lorav = k - ROPE
    nx = n // 2
    half = nx * hl
    heads = n * hl
    nc = nseq // G
    nq = nseq // GQ

    me = lax.axis_index('dcp')
    x = lax.div(me, 2)
    core = lax.rem(me, 2)
    right = lax.rem(me + 2, n)
    left = lax.rem(me + n - 2, n)
    opp = lax.rem(me + 4, n)
    mate = me + 1 - 2 * core

    def row(j):
        return (lax.rem(j, 2) * nx + lax.div(j, 2)) * hl

    def remote(src, dst, ssem, rsem, dev):
        return pltpu.make_async_remote_copy(
            src_ref=src, dst_ref=dst, send_sem=ssem, recv_sem=rsem, device_id={'dcp': dev},
            device_id_type=pl.DeviceIdType.MESH)

    def wait_on(ref, sem):
        pltpu.make_async_copy(ref, ref, sem).wait()

    def cache_copy(b):
        s = lax.rem(b, RING)
        return pltpu.make_async_copy(c_hbm.at[b], cbuf.at[s], csem.at[s])

    def qblk(c, j):
        return qall.at[pl.ds(c * GQ, GQ), pl.ds(row(j), hl), :]

    qcopy = pltpu.make_async_copy(q_hbm, qall.at[:, pl.ds(row(me), hl), :], lsem.at[0])
    qcopy.start()
    for b in range(EARLY * G):
        cache_copy(b).start()

    barrier = pltpu.get_barrier_semaphore()
    for d in range(1, n):
        pl.semaphore_signal(barrier, inc=1, device_id={'dcp': lax.rem(me + d, n)},
                            device_id_type=pl.DeviceIdType.MESH)
    pl.semaphore_wait(barrier, n - 1)
    qcopy.wait()

    def send_own(c):
        blk = qblk(c, me)
        remote(blk, blk, send_sem.at[0], ql_sem.at[c], right).start()
        remote(blk, blk, send_sem.at[1], qr_sem.at[c], left).start()
        remote(blk, blk, send_sem.at[2], qp_sem.at[c], mate).start()

    def q_first(c):
        wait_on(qblk(c, left), ql_sem.at[c])
        wait_on(qblk(c, right), qr_sem.at[c])
        even = lax.rem(c, 2) == 0
        blk = qblk(c, jnp.where(even, left, right))
        remote(blk, blk, send_sem.at[3], qd_sem.at[c], jnp.where(even, right, left)).start()
        for j in (left, right):
            blk = qblk(c, j)
            remote(blk, blk, send_sem.at[2], qp_sem.at[c], mate).start()

    def q_second(c):
        blk = qblk(c, opp)
        wait_on(blk, qd_sem.at[c])
        remote(blk, blk, send_sem.at[2], qp_sem.at[c], mate).start()

    def q_third(c):
        wait_on(qall.at[pl.ds(c * GQ, GQ), pl.ds((1 - core) * half, half), :], qp_sem.at[c])

    def score_dot(c, g):
        b = c * G + g
        ct = cbuf[lax.rem(b, RING)]
        ct = jnp.concatenate([ct[i] for i in range(npage)], axis=1)
        return lax.dot_general(qall[b], ct, (((1,), (0,)), ((), ())), preferred_element_type=jnp.float32)

    def softmax(c, g, s):
        b = c * G + g
        length = lens_ref[b] - me * npage
        posr = lax.broadcasted_iota(jnp.int32, (1, r), 1) * (n * npage)
        mask = jnp.concatenate([posr < length - i for i in range(npage)], axis=1)
        s = jnp.where(mask, s, -jnp.inf)
        m = jnp.max(s, axis=1, keepdims=True) * C2
        msafe = jnp.where(m == -jnp.inf, 0.0, m)
        p = jnp.exp2(s * C2 - msafe)
        l = jnp.sum(p, axis=1, keepdims=True)
        ps = lax.rem(b, PSLOT)
        pbuf[ps] = p
        mbuf[ps] = m
        lse = jnp.where(l > 0.0, msafe + jnp.log2(jnp.where(l > 0.0, l, 1.0)), -jnp.inf)
        t = jnp.transpose(jnp.broadcast_to(lse, (heads, heads)))
        lse_own[b] = t[0:1]

    def weigh(c, g):
        b = c * G + g
        u, v = lse_own[b], lse_mate[b]
        top = jnp.maximum(u, v)
        top = jnp.where(top == -jnp.inf, 0.0, top)
        big = top + jnp.log2(jnp.exp2(u - top) + jnp.exp2(v - top))
        lse_chip[b] = big
        big = jnp.where(big == -jnp.inf, 0.0, big)
        bigc = jnp.transpose(jnp.broadcast_to(big, (heads, heads)))[:, 0:1]
        ps = lax.rem(b, PSLOT)
        f = jnp.exp2(mbuf[ps] - bigc)
        abuf[g] = (pbuf[ps] * f).astype(jnp.bfloat16)

    def product_dot(c, g):
        b = c * G + g
        ct = cbuf[lax.rem(b, RING)]
        ct = jnp.concatenate([ct[i, :lorav] for i in range(npage)], axis=1)
        if NT:
            obuf[b] = lax.dot_general(abuf[g], ct, (((1,), (1,)), ((), ())), preferred_element_type=jnp.float32)
        else:
            ot = lax.dot_general(ct, abuf[g], (((1,), (1,)), ((), ())), preferred_element_type=jnp.float32)
            obuf[b] = jnp.transpose(ot)

    def arithmetic(cs, cp, cc, cf):
        if cc is not None:
            bs = pl.ds(cc * G, G)
            snd[bs] = (obuf[bs, pl.ds(core * half, half)] + xrecv[bs]).astype(jnp.bfloat16)
        if cp is not None:
            for g in range(G):
                weigh(cp, g)
        for g in range(G):
            if cs is not None:
                s = score_dot(cs, g)
            if cp is not None:
                product_dot(cp, g)
            if cs is not None:
                softmax(cs, g, s)
        if cf is not None:
            final(cf)

    def scores_wait(c):
        for g in range(G):
            cache_copy(c * G + g).wait()

    def product_wait(c):
        wait_on(lse_mate.at[pl.ds(c * G, G)], lse_sem.at[c])

    def scores_send(c):
        bs = pl.ds(c * G, G)
        remote(lse_own.at[bs], lse_mate.at[bs], send_sem.at[4], lse_sem.at[c], mate).start()

    def product_send(c):
        bs = pl.ds(c * G, G)
        remote(obuf.at[bs, pl.ds((1 - core) * half, half)], xrecv.at[bs], send_sem.at[5], x_sem.at[c],
               mate).start()
        for i, j in enumerate((right, left, opp)):
            remote(lse_chip.at[bs], lse_in.at[i, bs], send_sem.at[8], lc_sem.at[c], j).start()

    def prefetch(c):
        for g in range(G):
            cache_copy(c * G + g).start()

    def chip_wait(c):
        wait_on(xrecv.at[pl.ds(c * G, G)], x_sem.at[c])

    def chip_send(c):
        bs = pl.ds(c * G, G)

        def part(j):
            return snd.at[bs, pl.ds(lax.div(j, 2) * hl, hl)]

        even = lax.rem(c, 2) == 0
        remote(part(opp), relay_in.at[bs], send_sem.at[6], a_sem.at[c], jnp.where(even, right, left)).start()
        remote(part(right), o_in.at[0, bs], send_sem.at[6], ol_sem.at[c], right).start()
        remote(part(left), o_in.at[1, bs], send_sem.at[6], or_sem.at[c], left).start()

    def relay(c):
        bs = pl.ds(c * G, G)
        wait_on(relay_in.at[bs], a_sem.at[c])
        remote(relay_in.at[bs], o_in.at[2, bs], send_sem.at[7], od_sem.at[c],
               jnp.where(lax.rem(c, 2) == 0, right, left)).start()

    def final_wait(c):
        bs = pl.ds(c * G, G)
        wait_on(o_in.at[0, bs], ol_sem.at[c])
        wait_on(o_in.at[1, bs], or_sem.at[c])
        wait_on(o_in.at[2, bs], od_sem.at[c])
        wait_on(lse_in.at[:, bs], lc_sem.at[c])

    def final(c):
        rows = []
        for g in range(G):
            b = c * G + g
            z = [lse_chip[b]] + [lse_in[i, b] for i in range(3)]
            top = functools.reduce(jnp.maximum, z)
            z = [jnp.exp2(y - top) for y in z]
            tot = functools.reduce(jnp.add, z)
            rows += [y / tot for y in z]
        wt[...] = jnp.transpose(jnp.concatenate(rows, axis=0))
        w = wt[pl.ds(row(me), hl), :]
        for g in range(G):
            b = c * G + g
            o = (obuf[b, pl.ds(row(me), hl)] + xrecv[b, pl.ds(x * hl, hl)]) * w[:, 4 * g:4 * g + 1]
            for i in range(3):
                o += o_in[i, b].astype(jnp.float32) * w[:, 4 * g + 1 + i:4 * g + 2 + i]
            o_ref[b] = o.astype(o_ref.dtype)

    for c in range(AHEAD):
        send_own(c)

    def step(it, live):
        def stage(f, d, count=nc, skip=0):
            @pl.when((it >= d + skip) & (it < count + d))
            def _():
                f(it - d)

        @pl.when(it + AHEAD < nq)
        def _():
            send_own(it + AHEAD)

        stage(prefetch, D_SC - LEAD, nc, EARLY)
        stage(q_first, 0, nq)
        stage(q_second, D_Q2, nq)
        stage(q_third, D_Q3, nq)
        stage(relay, D_RL)
        cs, cp, cc, cf = [it - d if on else None for d, on in zip((D_SC, D_PR, D_CS, D_FI), live)]
        if cs is not None:
            scores_wait(cs)
        if cp is not None:
            product_wait(cp)
        if cc is not None:
            chip_wait(cc)
        if cf is not None:
            final_wait(cf)
        arithmetic(cs, cp, cc, cf)
        if cs is not None:
            scores_send(cs)
        if cp is not None:
            product_send(cp)
        if cc is not None:
            chip_send(cc)

    marks = sorted({0} | {d + e for d in (D_SC, D_PR, D_CS, D_FI) for e in (0, nc)})
    for lo, hi in zip(marks, marks[1:]):
        live = [d <= lo < d + nc for d in (D_SC, D_PR, D_CS, D_FI)]

        @pl.loop(lo, hi)
        def _(it, live=live):
            step(it, live)

    wait_on(qall.at[:, pl.ds(0, hl), :], send_sem.at[0])
    wait_on(qall.at[:, pl.ds(0, hl), :], send_sem.at[1])
    wait_on(qall.at[:, pl.ds(0, half), :], send_sem.at[2])
    wait_on(qall.at[:, pl.ds(0, hl), :], send_sem.at[3])
    wait_on(lse_own, send_sem.at[4])
    wait_on(lse_in, send_sem.at[8])
    wait_on(xrecv, send_sem.at[5])
    wait_on(snd.at[:, pl.ds(0, (nx - 1) * hl)], send_sem.at[6])
    wait_on(relay_in, send_sem.at[7])


def solution(mesh):
    n = mesh.shape['dcp']

    def local(q, cache, lens):
        b, hl, k = q.shape
        r = cache.shape[1]
        page = cache.shape[3]
        lorav = k - ROPE
        ct = cache.reshape(b, r, page, k).transpose(0, 2, 3, 1)
        heads = n * hl
        half = heads // 2
        nc = b // G
        dma = pltpu.SemaphoreType.DMA
        return pl.pallas_call(
            functools.partial(kernel, n),
            out_shape=jax.ShapeDtypeStruct((b, hl, lorav), jnp.bfloat16),
            in_specs=[pl.BlockSpec(memory_space=pl.ANY), pl.BlockSpec(memory_space=pl.ANY),
                      pl.BlockSpec(memory_space=pltpu.SMEM)],
            out_specs=pl.BlockSpec(memory_space=pltpu.VMEM),
            scratch_shapes=[
                pltpu.VMEM((b, heads, k), jnp.bfloat16),
                pltpu.VMEM((RING, page, k, r), jnp.bfloat16),
                pltpu.VMEM((PSLOT, heads, r * page), jnp.float32),
                pltpu.VMEM((G, heads, r * page), jnp.bfloat16),
                pltpu.VMEM((PSLOT, heads, 1), jnp.float32),
                pltpu.VMEM((b, 1, heads), jnp.float32),
                pltpu.VMEM((b, 1, heads), jnp.float32),
                pltpu.VMEM((b, 1, heads), jnp.float32),
                pltpu.VMEM((3, b, 1, heads), jnp.float32),
                pltpu.VMEM((heads, 4 * G), jnp.float32),
                pltpu.VMEM((b, heads, lorav), jnp.float32),
                pltpu.VMEM((b, half, lorav), jnp.float32),
                pltpu.VMEM((b, half, lorav), jnp.bfloat16),
                pltpu.VMEM((b, hl, lorav), jnp.bfloat16),
                pltpu.VMEM((3, b, hl, lorav), jnp.bfloat16),
                dma((1,)), dma((RING,)), dma((9,)),
            ] + [dma((b // GQ,))] * 4 + [dma((nc,))] * 7,
            compiler_params=pltpu.CompilerParams(
                collective_id=0, has_side_effects=True, vmem_limit_bytes=66_000_000),
        )(q, ct, lens)

    return jax.shard_map(local, mesh=mesh,
                         in_specs=(P('dp', 'dcp', None), P('dp', None, 'dcp', None, None), P('dp')),
                         out_specs=P('dp', 'dcp', None), check_vma=False)
```

time: 91.6 us -> 56.8 us (0.62)
  Pallas kernels: 88.9 us -> 54.6 us
    pallas_call x1, Pallas kernels: 88.9 us -> 54.6 us  [local(): pl.pallas_call(functools.partial(kernel, n), out_shape=jax.ShapeDtypeStru...]
where the time goes in v3:
time: 56.8 us; the launch traced here: 56.5 us
  Pallas kernels  54.6 us (96%)
  local copies, waits for them, and re-layouts  1.87 us (3%)
    pallas_call x1, Pallas kernels, local(): pl.pallas_call(functools.partial(kernel, n), out_shape=jax.ShapeDtypeStru...  54.6 us
    unnamed x1, local copies, waits for them, and re-layouts  1.87 us

profile of v3, /device:TPU:81, one launch (start us, length us, event | category | flops | bytes accessed | tf_op | source)
XLA Modules:
  0.0 56.5 jit_solution(4713236303387427117)
XLA Ops:
  0.0 54.6 %shard_map.37 = bf16[32,16,512]{2,1,0:T(8,128)(2,1)} custom-call(bf16[32,16,576]{2,1,0:T(8,128)(2,1)} %q_hbm.1, bf16[32,8,576,128]{3,2,1,0:T(8,128)(2,1)} %bitcast.3, s32[32]{0:T(128)} %lens_ref.1), custom_call_target="tpu_custom_call" | custom-call | tf_op jit(solution)/shard_map/pallas_call | solution.py:302
  54.6 1.9 %copy.5 = bf16[32,16,512]{2,1,0:T(8,128)(2,1)} copy(bf16[32,16,512]{2,1,0:T(8,128)(2,1)} %shard_map.37) | data formatting | bytes 1048576

commit v4 on v3

--- a/solution.py
+++ b/solution.py
@@ -12,9 +12,8 @@
 C2 = QK_DIM ** -0.5 * 1.4426950408889634
 
 G = 2
-GQ = 2
 AHEAD = 4
-RING = 14
+RING = 12
 PSLOT = 8
 LEAD = 3
 EARLY = 2
@@ -25,10 +24,10 @@
 D_CS = 10
 D_RL = 14
 D_FI = 19
-NT = True
-
-
-def kernel(n, q_hbm, c_hbm, lens_ref, o_ref, qall, cbuf, pbuf, abuf, mbuf, lse_own, lse_mate, lse_chip, lse_in, wt, obuf, xrecv, snd,
+NT = False
+
+
+def kernel(n, q_hbm, c_hbm, lens_hbm, o_ref, lens_ref, qloc, qall, cbuf, pbuf, abuf, mbuf, lse_own, lse_mate, lse_chip, lse_in, wt, obuf, xrecv, snd,
            relay_in, o_in, lsem, csem, send_sem, ql_sem, qr_sem, qd_sem, qp_sem, lse_sem, lc_sem, x_sem,
            a_sem, ol_sem, or_sem, od_sem):
     nseq, hl, k = q_hbm.shape
@@ -38,7 +37,7 @@
     half = nx * hl
     heads = n * hl
     nc = nseq // G
-    nq = nseq // GQ
+    nq = nc
 
     me = lax.axis_index('dcp')
     x = lax.div(me, 2)
@@ -64,10 +63,12 @@
         return pltpu.make_async_copy(c_hbm.at[b], cbuf.at[s], csem.at[s])
 
     def qblk(c, j):
-        return qall.at[pl.ds(c * GQ, GQ), pl.ds(row(j), hl), :]
-
-    qcopy = pltpu.make_async_copy(q_hbm, qall.at[:, pl.ds(row(me), hl), :], lsem.at[0])
+        return qall.at[c, pl.ds(row(j), hl), :]
+
+    qcopy = pltpu.make_async_copy(q_hbm, qloc, lsem.at[0])
     qcopy.start()
+    lcopy = pltpu.make_async_copy(lens_hbm, lens_ref, lsem.at[1])
+    lcopy.start()
     for b in range(EARLY * G):
         cache_copy(b).start()
 
@@ -75,8 +76,13 @@
     for d in range(1, n):
         pl.semaphore_signal(barrier, inc=1, device_id={'dcp': lax.rem(me + d, n)},
                             device_id_type=pl.DeviceIdType.MESH)
+    qcopy.wait()
+    lcopy.wait()
+    for c in range(nq):
+        u, v = qloc[2 * c], qloc[2 * c + 1]
+        qall[c, pl.ds(row(me), hl), :] = jnp.concatenate(
+            [u[:, :lorav], v[:, :lorav], u[:, lorav:], v[:, lorav:]], axis=1)
     pl.semaphore_wait(barrier, n - 1)
-    qcopy.wait()
 
     def send_own(c):
         blk = qblk(c, me)
@@ -100,13 +106,17 @@
         remote(blk, blk, send_sem.at[2], qp_sem.at[c], mate).start()
 
     def q_third(c):
-        wait_on(qall.at[pl.ds(c * GQ, GQ), pl.ds((1 - core) * half, half), :], qp_sem.at[c])
+        wait_on(qall.at[c, pl.ds((1 - core) * half, half), :], qp_sem.at[c])
 
     def score_dot(c, g):
         b = c * G + g
         ct = cbuf[lax.rem(b, RING)]
         ct = jnp.concatenate([ct[i] for i in range(npage)], axis=1)
-        return lax.dot_general(qall[b], ct, (((1,), (0,)), ((), ())), preferred_element_type=jnp.float32)
+        zero = jnp.zeros((k - lorav, ct.shape[1]), ct.dtype)
+        ct = jnp.concatenate([ct, zero] if g == 0 else [ct[:lorav], zero, ct[lorav:]], axis=0)
+        q = qall[c]
+        q = jnp.concatenate([q[:, g * lorav:(g + 1) * lorav], q[:, 2 * lorav:]], axis=1)
+        return lax.dot_general(q, ct, (((1,), (0,)), ((), ())), preferred_element_type=jnp.float32)
 
     def softmax(c, g, s):
         b = c * G + g
@@ -302,11 +312,13 @@
         return pl.pallas_call(
             functools.partial(kernel, n),
             out_shape=jax.ShapeDtypeStruct((b, hl, lorav), jnp.bfloat16),
-            in_specs=[pl.BlockSpec(memory_space=pl.ANY), pl.BlockSpec(memory_space=pl.ANY),
-                      pl.BlockSpec(memory_space=pltpu.SMEM)],
+            in_specs=[pl.BlockSpec(memory_space=pltpu.HBM), pl.BlockSpec(memory_space=pltpu.HBM),
+                      pl.BlockSpec(memory_space=pltpu.HBM)],
             out_specs=pl.BlockSpec(memory_space=pltpu.VMEM),
             scratch_shapes=[
-                pltpu.VMEM((b, heads, k), jnp.bfloat16),
+                pltpu.SMEM((b,), jnp.int32),
+                pltpu.VMEM((b, hl, k), jnp.bfloat16),
+                pltpu.VMEM((nc, heads, 2 * k), jnp.bfloat16),
                 pltpu.VMEM((RING, page, k, r), jnp.bfloat16),
                 pltpu.VMEM((PSLOT, heads, r * page), jnp.float32),
                 pltpu.VMEM((G, heads, r * page), jnp.bfloat16),
@@ -321,10 +333,10 @@
                 pltpu.VMEM((b, half, lorav), jnp.bfloat16),
                 pltpu.VMEM((b, hl, lorav), jnp.bfloat16),
                 pltpu.VMEM((3, b, hl, lorav), jnp.bfloat16),
-                dma((1,)), dma((RING,)), dma((9,)),
-            ] + [dma((b // GQ,))] * 4 + [dma((nc,))] * 7,
+                dma((2,)), dma((RING,)), dma((9,)),
+            ] + [dma((nc,))] * 11,
             compiler_params=pltpu.CompilerParams(
-                collective_id=0, has_side_effects=True, vmem_limit_bytes=66_000_000),
+                collective_id=0, has_side_effects=True, vmem_limit_bytes=56_000_000),
         )(q, ct, lens)
 
     return jax.shard_map(local, mesh=mesh,

time: 56.8 us -> 52.8 us (0.930)
  Pallas kernels: 54.6 us -> 51.3 us
    pallas_call x1, Pallas kernels: 54.6 us -> 51.3 us  [local(): pl.pallas_call(functools.partial(kernel, n), out_shape=jax.ShapeDtypeStru...]
    unnamed x1 -> x3, local copies, waits for them, and re-layouts: 1.87 us -> 1.45 us
where the time goes in v4:
time: 52.8 us; the launch traced here: 52.7 us
  Pallas kernels  51.3 us (97%)
  local copies, waits for them, and re-layouts  1.45 us (3%)
    pallas_call x1, Pallas kernels, local(): pl.pallas_call(functools.partial(kernel, n), out_shape=jax.ShapeDtypeStru...  51.3 us
    unnamed x3, local copies, waits for them, and re-layouts  1.45 us

profile of v4, /device:TPU:81, one launch (start us, length us, event | category | flops | bytes accessed | tf_op | source)
XLA Modules:
  0.0 52.7 jit_solution(8281639469748598227)
XLA Ops:
  0.0 0.0 copy-start
  0.0 0.7 %copy-done = s32[32]{0:T(128)S(1)} copy-done((s32[32]{0:T(128)S(1)}, s32[32]{0:T(128)}, u32[]{:S(2)}) %copy-start) | copy-done | bytes 152
  0.7 51.3 %shard_map.37 = bf16[32,16,512]{2,1,0:T(8,128)(2,1)S(1)} custom-call(bf16[32,16,576]{2,1,0:T(8,128)(2,1)} %q_hbm.1, bf16[32,8,576,128]{3,2,1,0:T(8,128)(2,1)} %bitcast.3, s32[32]{0:T(128)S(1)} %copy-done), custom_call_target="tpu_custom_call" | custom-call | tf_op jit(solution)/shard_map/pallas_call | solution.py:312
  51.9 0.8 %copy.5 = bf16[32,16,512]{2,1,0:T(8,128)(2,1)} copy(bf16[32,16,512]{2,1,0:T(8,128)(2,1)S(1)} %shard_map.37) | data formatting | bytes 1048576
Async XLA Ops:
  0.0 0.7 %copy-start = (s32[32]{0:T(128)S(1)}, s32[32]{0:T(128)}, u32[]{:S(2)}) copy-start(s32[32]{0:T(128)} %lens_hbm.1) | copy-start | bytes 388

commit v5 on v4

--- a/solution.py
+++ b/solution.py
@@ -15,6 +15,7 @@
 AHEAD = 4
 RING = 12
 PSLOT = 8
+LG = 4
 LEAD = 3
 EARLY = 2
 D_Q2 = 4
@@ -22,8 +23,8 @@
 D_SC = 6
 D_PR = 8
 D_CS = 10
-D_RL = 14
-D_FI = 19
+D_RL = 15
+D_FI = 20
 NT = False
 
 
@@ -141,12 +142,13 @@
         top = jnp.maximum(u, v)
         top = jnp.where(top == -jnp.inf, 0.0, top)
         big = top + jnp.log2(jnp.exp2(u - top) + jnp.exp2(v - top))
-        lse_chip[b] = big
+        whole = big
         big = jnp.where(big == -jnp.inf, 0.0, big)
         bigc = jnp.transpose(jnp.broadcast_to(big, (heads, heads)))[:, 0:1]
         ps = lax.rem(b, PSLOT)
         f = jnp.exp2(mbuf[ps] - bigc)
         abuf[g] = (pbuf[ps] * f).astype(jnp.bfloat16)
+        return whole
 
     def product_dot(c, g):
         b = c * G + g
@@ -163,8 +165,11 @@
             bs = pl.ds(cc * G, G)
             snd[bs] = (obuf[bs, pl.ds(core * half, half)] + xrecv[bs]).astype(jnp.bfloat16)
         if cp is not None:
-            for g in range(G):
-                weigh(cp, g)
+            u, v = [weigh(cp, g) for g in range(G)]
+            u = jnp.where(core == 0, u, jnp.roll(u, half, axis=1))
+            v = jnp.where(core == 0, jnp.roll(v, half, axis=1), v)
+            lane = lax.broadcasted_iota(jnp.int32, (1, heads), 1)
+            lse_chip[cp] = jnp.where(lane < half, u, v)
         for g in range(G):
             if cs is not None:
                 s = score_dot(cs, g)
@@ -190,8 +195,12 @@
         bs = pl.ds(c * G, G)
         remote(obuf.at[bs, pl.ds((1 - core) * half, half)], xrecv.at[bs], send_sem.at[5], x_sem.at[c],
                mate).start()
-        for i, j in enumerate((right, left, opp)):
-            remote(lse_chip.at[bs], lse_in.at[i, bs], send_sem.at[8], lc_sem.at[c], j).start()
+
+        @pl.when(lax.rem(c, LG) == LG - 1)
+        def _():
+            cs = pl.ds(c - (LG - 1), LG)
+            for i, j in enumerate((right, left, opp)):
+                remote(lse_chip.at[cs], lse_in.at[i, cs], send_sem.at[8], lc_sem.at[lax.div(c, LG)], j).start()
 
     def prefetch(c):
         for g in range(G):
@@ -206,40 +215,40 @@
         def part(j):
             return snd.at[bs, pl.ds(lax.div(j, 2) * hl, hl)]
 
-        even = lax.rem(c, 2) == 0
-        remote(part(opp), relay_in.at[bs], send_sem.at[6], a_sem.at[c], jnp.where(even, right, left)).start()
+        remote(part(opp), relay_in.at[bs], send_sem.at[6], a_sem.at[c], onward(c)).start()
         remote(part(right), o_in.at[0, bs], send_sem.at[6], ol_sem.at[c], right).start()
         remote(part(left), o_in.at[1, bs], send_sem.at[6], or_sem.at[c], left).start()
 
+    def onward(c):
+        return jnp.where(lax.rem(c, 2) == 0, right, left)
+
     def relay(c):
         bs = pl.ds(c * G, G)
         wait_on(relay_in.at[bs], a_sem.at[c])
-        remote(relay_in.at[bs], o_in.at[2, bs], send_sem.at[7], od_sem.at[c],
-               jnp.where(lax.rem(c, 2) == 0, right, left)).start()
+        remote(relay_in.at[bs], o_in.at[2, bs], send_sem.at[7], od_sem.at[c], onward(c)).start()
 
     def final_wait(c):
         bs = pl.ds(c * G, G)
         wait_on(o_in.at[0, bs], ol_sem.at[c])
         wait_on(o_in.at[1, bs], or_sem.at[c])
         wait_on(o_in.at[2, bs], od_sem.at[c])
-        wait_on(lse_in.at[:, bs], lc_sem.at[c])
+
+        @pl.when(lax.rem(c, LG) == 0)
+        def _():
+            wait_on(lse_in.at[:, pl.ds(c, LG)], lc_sem.at[lax.div(c, LG)])
 
     def final(c):
-        rows = []
+        z = [lse_chip[c]] + [lse_in[i, c] for i in range(3)]
+        top = functools.reduce(jnp.maximum, z)
+        z = [jnp.exp2(y - top) for y in z]
+        tot = functools.reduce(jnp.add, z)
+        wt[...] = jnp.transpose(jnp.concatenate([y / tot for y in z + z], axis=0))
         for g in range(G):
             b = c * G + g
-            z = [lse_chip[b]] + [lse_in[i, b] for i in range(3)]
-            top = functools.reduce(jnp.maximum, z)
-            z = [jnp.exp2(y - top) for y in z]
-            tot = functools.reduce(jnp.add, z)
-            rows += [y / tot for y in z]
-        wt[...] = jnp.transpose(jnp.concatenate(rows, axis=0))
-        w = wt[pl.ds(row(me), hl), :]
-        for g in range(G):
-            b = c * G + g
-            o = (obuf[b, pl.ds(row(me), hl)] + xrecv[b, pl.ds(x * hl, hl)]) * w[:, 4 * g:4 * g + 1]
+            w = wt[pl.ds(g * half + x * hl, hl), :]
+            o = (obuf[b, pl.ds(row(me), hl)] + xrecv[b, pl.ds(x * hl, hl)]) * w[:, 0:1]
             for i in range(3):
-                o += o_in[i, b].astype(jnp.float32) * w[:, 4 * g + 1 + i:4 * g + 2 + i]
+                o += o_in[i, b].astype(jnp.float32) * w[:, 1 + i:2 + i]
             o_ref[b] = o.astype(o_ref.dtype)
 
     for c in range(AHEAD):
@@ -325,9 +334,9 @@
                 pltpu.VMEM((PSLOT, heads, 1), jnp.float32),
                 pltpu.VMEM((b, 1, heads), jnp.float32),
                 pltpu.VMEM((b, 1, heads), jnp.float32),
-                pltpu.VMEM((b, 1, heads), jnp.float32),
-                pltpu.VMEM((3, b, 1, heads), jnp.float32),
-                pltpu.VMEM((heads, 4 * G), jnp.float32),
+                pltpu.VMEM((nc, 1, heads), jnp.float32),
+                pltpu.VMEM((3, nc, 1, heads), jnp.float32),
+                pltpu.VMEM((heads, 8), jnp.float32),
                 pltpu.VMEM((b, heads, lorav), jnp.float32),
                 pltpu.VMEM((b, half, lorav), jnp.float32),
                 pltpu.VMEM((b, half, lorav), jnp.bfloat16),

time: 52.8 us -> 52 us (0.985)
  Pallas kernels: 51.3 us -> 50.4 us
    pallas_call x1, Pallas kernels: 51.3 us -> 50.4 us  [local(): pl.pallas_call(functools.partial(kernel, n), out_shape=jax.ShapeDtypeStru...]
where the time goes in v5:
time: 52 us; the launch traced here: 51.9 us
  Pallas kernels  50.4 us (97%)
  local copies, waits for them, and re-layouts  1.45 us (3%)
    pallas_call x1, Pallas kernels, local(): pl.pallas_call(functools.partial(kernel, n), out_shape=jax.ShapeDtypeStru...  50.4 us
    unnamed x3, local copies, waits for them, and re-layouts  1.45 us

profile of v5, /device:TPU:81, one launch (start us, length us, event | category | flops | bytes accessed | tf_op | source)
XLA Modules:
  0.0 51.9 jit_solution(888744609717962213)
XLA Ops:
  0.0 0.0 copy-start
  0.0 0.7 %copy-done = s32[32]{0:T(128)S(1)} copy-done((s32[32]{0:T(128)S(1)}, s32[32]{0:T(128)}, u32[]{:S(2)}) %copy-start) | copy-done | bytes 152
  0.7 50.4 %shard_map.37 = bf16[32,16,512]{2,1,0:T(8,128)(2,1)S(1)} custom-call(bf16[32,16,576]{2,1,0:T(8,128)(2,1)} %q_hbm.1, bf16[32,8,576,128]{3,2,1,0:T(8,128)(2,1)} %bitcast.3, s32[32]{0:T(128)S(1)} %copy-done), custom_call_target="tpu_custom_call" | custom-call | tf_op jit(solution)/shard_map/pallas_call | solution.py:321
  51.1 0.8 %copy.5 = bf16[32,16,512]{2,1,0:T(8,128)(2,1)} copy(bf16[32,16,512]{2,1,0:T(8,128)(2,1)S(1)} %shard_map.37) | data formatting | bytes 1048576
Async XLA Ops:
  0.0 0.7 %copy-start = (s32[32]{0:T(128)S(1)}, s32[32]{0:T(128)}, u32[]{:S(2)}) copy-start(s32[32]{0:T(128)} %lens_hbm.1) | copy-start | bytes 388
